TPU v7x, 32 devices: a whole 2x2x4 slice. The times are simulated.
32 devices in a mesh: subset: 8 (over z, x), vocab: 4 (over y, core).
Axes of the slice: x: 2, y: 2, z: 4, core: 2. Of those that a mesh axis runs over, the one named last changes fastest.
Arguments:
- hidden: bfloat16 [4096, 2048], P('subset', 'vocab'), may hold values from -100 to 100
- proj_weight: bfloat16 [2048, 25600], P('subset', 'vocab'), may hold values from -1 to 1
- targets: int32 [4096], P('subset'), may hold values from 0 to 25599
- counts: int32 [8, 100, 512], P('subset', 'vocab'), may hold values from 1 to 15, as said below
- ranks: int32 [8], replicated, may hold values from 0 to 799
Outputs:
- row_cross_entropy: float32 [4096], P('subset')
- resample_mean_losses: float32 [8, 100], P('subset', 'vocab')
- quantiles: float32 [8], replicated
Inputs may be any that keep to these rules, and one draw needn't show every extreme that they name: For every subset and resample the counts over the 512 rows sum to 4096.
All inputs are finite; a program needn't handle non-finite values.
Results may differ from a plain program's by a relative error of at most 0.0003.
Values may be sent and summed in bfloat16 or wider, within the bound.
No kernel may reach another device: no remote copies, remote signals or barrier semaphores. Data moves between devices by JAX's collectives and lax.ppermute only.
A program may use at most 128 MiB of HBM per device.

v0:
```python
import jax
import jax.numpy as jnp
from jax import lax
from jax.sharding import PartitionSpec as P


def shards(hidden, proj_weight, targets, counts, ranks):
    features = lax.all_gather(hidden, "vocab", axis=1, tiled=True)
    columns = proj_weight.shape[1]
    whole_weight = lax.all_gather(proj_weight, "subset", axis=0, tiled=True)
    logit_scores = jnp.dot(features, whole_weight, preferred_element_type=jnp.float32)
    local_top = jnp.max(logit_scores, axis=1)
    local_sum = jnp.sum(jnp.exp(logit_scores - local_top[:, None]), axis=1)
    offset = targets - lax.axis_index("vocab") * columns
    inside = (offset >= 0) & (offset < columns)
    picked = jnp.take_along_axis(logit_scores, jnp.clip(offset, 0, columns - 1)[:, None], axis=1)[
        :, 0
    ]
    picked = jnp.where(inside, picked, 0.0)
    row_max = lax.pmax(local_top, "vocab")
    row_total, target_logit = lax.psum((local_sum * jnp.exp(local_top - row_max), picked), "vocab")
    row_cross_entropy = row_max + jnp.log(row_total) - target_logit
    total_rows = 1.0 * lax.axis_size("subset") * row_cross_entropy.shape[0]
    resample_mean_losses = (
        jnp.einsum(
            "cno,o->cn",
            counts.astype(jnp.float32),
            row_cross_entropy,
            precision=lax.Precision.HIGHEST,
        )
        / total_rows
    )
    grouped = lax.all_gather(resample_mean_losses, "vocab", axis=1, tiled=True)
    gathered = lax.all_gather(grouped, "subset", axis=0, tiled=True)
    pooled = jnp.sort(gathered.reshape(-1))
    positions = lax.iota(jnp.int32, pooled.shape[0])
    chosen = positions[:, None] == ranks[None, :]
    quantiles = jnp.sum(jnp.where(chosen, pooled[:, None], 0.0), axis=0)
    return (row_cross_entropy, resample_mean_losses, quantiles)


def solution(mesh):
    return jax.shard_map(
        shards,
        mesh=mesh,
        in_specs=(
            P("subset", "vocab"),
            P("subset", "vocab"),
            P("subset"),
            P("subset", "vocab", None),
            P(),
        ),
        out_specs=(P("subset"), P("subset", "vocab"), P()),
        check_vma=False,
    )
```

profile of v0, /device:TPU:0, one launch (start us, length us, event | category | flops | bytes accessed | tf_op | source)
XLA Modules:
  0.0 625.1 jit_solution(13795552494358012324)
XLA Ops:
  7.2 0.0 all-gather.5.cloned.1.call-start
  7.2 0.7 all-gather.5.cloned.1.call-update
  7.9 0.0 all-gather.7.cloned.1.call-start
  7.9 0.7 all-gather.7.cloned.1.call-update
  8.7 0.8 convert_element_type.3
  9.5 1.2 dynamic-slice
  10.8 1.2 dynamic-slice.1
  13.3 0.7 compare_select_fusion
  14.0 20.8 %all-gather.5.cloned.1.call-done = bf16[512,2048]{1,0:T(8,128)(2,1)} async-done(((bf16[512,512]{1,0:T(8,128)(2,1)}), bf16[512,2048]{1,0:T(8,128)(2,1)}) %all-gather.5.cloned.1.call-update) | async-done | bytes 2097168 | tf_op jit(solution)/shard_map/all_gather | solution.py:8
  34.9 501.6 %all-gather.7.cloned.1.call-done = bf16[2048,6400]{1,0:T(8,128)(2,1)} async-done(((bf16[256,6400]{1,0:T(8,128)(2,1)}), bf16[2048,6400]{1,0:T(8,128)(2,1)}) %all-gather.7.cloned.1.call-update) | async-done | bytes 26214416 | tf_op jit(solution)/shard_map/all_gather | solution.py:10
  536.4 22.5 %fusion.6 = (f32[512]{0:T(512)S(1)}, f32[512,6400]{1,0:T(8,128)}) fusion(bf16[512,2048]{1,0:T(8,128)(2,1)} %all-gather.5.cloned.1.call-done, bf16[2048,6400]{1,0:T(8,128)(2,1)} %all-gather.7.cloned.1.call-done), kind=kOutput, calls=%fused_computation.18 | convolution fusion | flops 13425049600 | bytes 41420800 | tf_op jit(solution)/shard_map/dot_general | solution.py:11
  558.9 0.0 copy-start
  558.9 0.0 copy-start.3
  558.9 6.5 %pmax.7 = f32[512]{0:T(512)S(1)} all-reduce(f32[512]{0:T(512)S(1)} %get-tuple-element.8), channel_id=1, replica_groups=mesh['subset'=8,'vocab'=4] {'vocab'}, use_global_device_ids=true, to_apply=%region_1.0 | all-reduce | flops 512 | bytes 4096 | tf_op jit(solution)/shard_map/pmax | solution.py:20
  565.5 6.6 %exponential_reduce_fusion = f32[512]{0:T(512)S(1)} fusion(f32[512,6400]{1,0:T(8,128)} %get-tuple-element.9, f32[512]{0:T(512)S(1)} %get-tuple-element.8), kind=kLoop, calls=%fused_computation.1 | loop fusion | flops 6553088 | bytes 13111296 | tf_op jit(solution)/shard_map/reduce_sum | solution.py:13
  572.0 8.2 %gather_fusion = f32[512]{0:T(512)S(1)} fusion(f32[512,6400]{1,0:T(8,128)} %get-tuple-element.9, s32[512]{0:T(512)S(1)} %bitcast.18), kind=kCustom, calls=%fused_computation | custom fusion | bytes 8192 | tf_op jit(solution)/shard_map/jit(take_along_axis)/gather | solution.py:16
  580.2 0.0 copy-done
  580.2 5.8 all-reduce.2
  586.1 0.0 copy-start.1
  586.1 0.1 fusion
  586.2 0.0 copy-start.2
  586.3 0.2 dynamic-update-slice
  586.5 5.7 all-reduce
  592.3 0.2 dynamic-update-slice.1
  592.5 20.5 %all-reduce.1 = f32[800]{0:T(1024)S(1)} all-reduce(f32[800]{0:T(1024)S(1)} %dynamic-update-slice.1), channel_id=3, replica_groups=mesh['subset'=8,'vocab'=4] {'subset'}, use_global_device_ids=true, to_apply=%add.1 | all-reduce | flops 800 | bytes 6400
  613.0 4.5 sort.15
  617.5 0.0 copy-done.3
  617.6 0.7 select_reduce_fusion
  618.3 0.0 copy-done.1
  618.3 0.0 copy-done.2
  (9 shorter events, 0.1 us)
Async XLA Ops:
  7.2 27.7 %all-gather.5.cloned.1.call-start = ((), (), s32[]{:S(2)}) async-start(), calls=%async_computation | async-start | bytes 2621440 | tf_op jit(solution)/shard_map/all_gather | solution.py:8
  7.9 528.6 %all-gather.7.cloned.1.call-start = ((), (), s32[]{:S(2)}) async-start(), calls=%async_computation.1 | async-start | bytes 29491200 | tf_op jit(solution)/shard_map/all_gather | solution.py:10
  558.9 21.3 %copy-start = (s32[512]{0:T(512)S(1)}, s32[512]{0:T(512)}, u32[]{:S(2)}) copy-start(s32[512]{0:T(512)} %param.7) | copy-start | bytes 6148
  558.9 58.6 %copy-start.3 = (s32[8]{0:T(128)S(1)}, s32[8]{0:T(128)}, u32[]{:S(2)}) copy-start(s32[8]{0:T(128)} %param.9) | copy-start | bytes 100
  586.1 32.2 %copy-start.1 = (f32[512]{0:T(512)}, f32[512]{0:T(512)S(1)}, u32[]{:S(2)}) copy-start(f32[512]{0:T(512)S(1)} %add_subtract_fusion) | copy-start | bytes 6148
  586.2 32.0 %copy-start.2 = (f32[25]{0:T(128)}, f32[25]{0:T(128)S(1)}, u32[]{:S(2)}) copy-start(f32[25]{0:T(128)S(1)} %fusion) | copy-start | bytes 304
Sparse Core Ops, SparseCore 0:
  9.5 25.2 all-gather.4
  36.4 500.0 all-gather.6
where the time goes:
time: 626 us; the launch traced here: 625 us
  waiting for transfers between devices  524 us (84%)
  blocking collectives  38.6 us (6%)
  matrix products  22.6 us (4%)
  between operations  15.4 us (2%)
  other arithmetic  13.4 us (2%)
  local copies, waits for them, and re-layouts  11.1 us (2%)
    all_gather x1, waiting for transfers between devices, shards(): whole_weight = lax.all_gather(proj_weight, 'subset', axis=0, tiled=True)  502 us
    unnamed x2, blocking collectives  26.3 us
    dot_general x1, matrix products, shards(): jnp.dot(features, whole_weight, preferred_element_type=jnp.float32)  22.5 us
    all_gather x1, waiting for transfers between devices, shards(): features = lax.all_gather(hidden, 'vocab', axis=1, tiled=True)  20.8 us
  transfers between devices with their start and end apart: 2, of which 2 were waited for; matrix products, arithmetic and copies ran while one was open for 1% of the time, Pallas kernels for 0%

commit v1 on v0

--- a/solution.py
+++ b/solution.py
@@ -7,7 +7,14 @@
 def shards(hidden, proj_weight, targets, counts, ranks):
     features = lax.all_gather(hidden, "vocab", axis=1, tiled=True)
     columns = proj_weight.shape[1]
-    whole_weight = lax.all_gather(proj_weight, "subset", axis=0, tiled=True)
+    ring = [proj_weight]
+    for hop in range(7):
+        ring.append(lax.ppermute(ring[-1], "subset", [(dev, (dev + 1) % 8) for dev in range(8)]))
+    whole_weight = jnp.roll(
+        jnp.concatenate(ring[::-1], axis=0),
+        (lax.axis_index("subset") + 1) * ring[0].shape[0],
+        axis=0,
+    )
     logit_scores = jnp.dot(features, whole_weight, preferred_element_type=jnp.float32)
     local_top = jnp.max(logit_scores, axis=1)
     local_sum = jnp.sum(jnp.exp(logit_scores - local_top[:, None]), axis=1)

time: 626 us -> 675 us (1.078)
  local copies, waits for them, and re-layouts: 11.1 us -> 80 us
  waiting for transfers between devices: 524 us -> 504 us
    ppermute x0 -> x7, waiting for transfers between devices: none -> 504 us  [shards(): lax.ppermute(ring[-1], 'subset', [(dev, (dev + 1) % 8) for dev in range(8)])]
    all_gather x1 -> x0, waiting for transfers between devices: 502 us -> none  [shards(): whole_weight = lax.all_gather(proj_weight, 'subset', axis=0, tiled=True)]
    unnamed x15 -> x52, local copies, waits for them, and re-layouts: 2.99 us -> 59.5 us
    all_gather x1, waiting for transfers between devices: 20.8 us -> 0.01 us  [shards(): features = lax.all_gather(hidden, 'vocab', axis=1, tiled=True)]
    gather x1, local copies, waits for them, and re-layouts: 8.15 us -> 18.6 us  [shards(): jnp.take_along_axis(logit_scores, jnp.clip(offset, 0, columns - 1)[:, Non...]
  transfers between devices with their start and end apart: 2 -> 8, of which waited for: 2 -> 7; matrix products, arithmetic and copies ran while one was open for 1% -> 8% of each run, Pallas kernels for 0% -> 0%
where the time goes in v1:
time: 675 us; the launch traced here: 674 us
  waiting for transfers between devices  504 us (75%)
  local copies, waits for them, and re-layouts  80 us (12%)
  blocking collectives  34.5 us (5%)
  matrix products  22.5 us (3%)
  between operations  16 us (2%)
  other arithmetic  14.2 us (2%)
    ppermute x7, waiting for transfers between devices, shards(): lax.ppermute(ring[-1], 'subset', [(dev, (dev + 1) % 8) for dev in range(8)])  504 us
    unnamed x52, local copies, waits for them, and re-layouts  59.5 us
    unnamed x2, blocking collectives  22.9 us
    dot_general x1, matrix products, shards(): jnp.dot(features, whole_weight, preferred_element_type=jnp.float32)  22.4 us
    gather x1, local copies, waits for them, and re-layouts, shards(): jnp.take_along_axis(logit_scores, jnp.clip(offset, 0, columns - 1)[:, Non...  18.6 us
  transfers between devices with their start and end apart: 8, of which 7 were waited for; matrix products, arithmetic and copies ran while one was open for 8% of the time, Pallas kernels for 0%

profile of v1, /device:TPU:0, one launch (start us, length us, event | category | flops | bytes accessed | tf_op | source)
XLA Modules:
  0.0 673.8 jit_solution(649817708830700547)
XLA Ops:
  7.2 0.0 copy-start
  7.2 0.0 all-gather.4.cloned.1.call-start
  7.2 3.0 collective-permute-start
  10.2 74.2 %collective-permute-done = bf16[256,6400]{1,0:T(8,128)(2,1)S(1)} collective-permute-done((bf16[256,6400]{1,0:T(8,128)(2,1)}, bf16[256,6400]{1,0:T(8,128)(2,1)S(1)}, u32[]{:S(2)}, u32[]{:S(2)}) %collective-permute-start) | collective-permute-done | bytes 3276832 | tf_op jit(solution)/shard_map/ppermute | solution.py:12
  84.4 1.7 copy-done.1
  86.1 0.0 collective-permute-start.1
  86.1 74.8 %collective-permute-done.1 = bf16[256,6400]{1,0:T(8,128)(2,1)S(1)} collective-permute-done((bf16[256,6400]{1,0:T(8,128)(2,1)S(1)}, bf16[256,6400]{1,0:T(8,128)(2,1)S(1)}, u32[]{:S(2)}, u32[]{:S(2)}) %collective-permute-start.1) | collective-permute-done | bytes 3276832 | tf_op jit(solution)/shard_map/ppermute | solution.py:12
  160.9 1.7 copy-done.3
  162.6 0.0 collective-permute-start.2
  162.6 73.9 %collective-permute-done.2 = bf16[256,6400]{1,0:T(8,128)(2,1)S(1)} collective-permute-done((bf16[256,6400]{1,0:T(8,128)(2,1)S(1)}, bf16[256,6400]{1,0:T(8,128)(2,1)S(1)}, u32[]{:S(2)}, u32[]{:S(2)}) %collective-permute-start.2) | collective-permute-done | bytes 3276832 | tf_op jit(solution)/shard_map/ppermute | solution.py:12
  236.5 1.7 copy-done.5
  238.2 0.0 collective-permute-start.3
  238.2 73.1 %collective-permute-done.3 = bf16[256,6400]{1,0:T(8,128)(2,1)S(1)} collective-permute-done((bf16[256,6400]{1,0:T(8,128)(2,1)S(1)}, bf16[256,6400]{1,0:T(8,128)(2,1)S(1)}, u32[]{:S(2)}, u32[]{:S(2)}) %collective-permute-start.3) | collective-permute-done | bytes 3276832 | tf_op jit(solution)/shard_map/ppermute | solution.py:12
  311.3 1.7 copy-done.7
  313.0 0.0 collective-permute-start.4
  313.0 72.2 %collective-permute-done.4 = bf16[256,6400]{1,0:T(8,128)(2,1)S(1)} collective-permute-done((bf16[256,6400]{1,0:T(8,128)(2,1)S(1)}, bf16[256,6400]{1,0:T(8,128)(2,1)S(1)}, u32[]{:S(2)}, u32[]{:S(2)}) %collective-permute-start.4) | collective-permute-done | bytes 3276832 | tf_op jit(solution)/shard_map/ppermute | solution.py:12
  385.2 1.7 copy-done.9
  386.9 0.0 collective-permute-start.5
  386.9 71.4 %collective-permute-done.5 = bf16[256,6400]{1,0:T(8,128)(2,1)} collective-permute-done((bf16[256,6400]{1,0:T(8,128)(2,1)S(1)}, bf16[256,6400]{1,0:T(8,128)(2,1)}, u32[]{:S(2)}, u32[]{:S(2)}) %collective-permute-start.5) | collective-permute-done | bytes 3276832 | tf_op jit(solution)/shard_map/ppermute | solution.py:12
  458.4 0.0 collective-permute-start.6
  458.4 0.0 all-gather.4.cloned.1.call-update
  458.4 0.8 convert_element_type.3
  459.3 1.2 dynamic-slice
  460.5 1.2 dynamic-slice.1
  461.8 0.0 copy-start.2
  463.6 1.6 compare_select_fusion
  465.2 64.0 %collective-permute-done.6 = bf16[256,6400]{1,0:T(8,128)(2,1)} collective-permute-done((bf16[256,6400]{1,0:T(8,128)(2,1)}, bf16[256,6400]{1,0:T(8,128)(2,1)}, u32[]{:S(2)}, u32[]{:S(2)}) %collective-permute-start.6) | collective-permute-done | bytes 3276832 | tf_op jit(solution)/shard_map/ppermute | solution.py:12
  529.2 3.8 constant_dynamic-update-slice_fusion.15
  533.0 3.9 constant_dynamic-update-slice_fusion.14
  536.8 3.9 constant_dynamic-update-slice_fusion.13
  540.7 3.9 constant_dynamic-update-slice_fusion.12
  544.6 3.8 constant_dynamic-update-slice_fusion.11
  548.4 3.8 constant_dynamic-update-slice_fusion.10
  552.2 3.9 constant_dynamic-update-slice_fusion.9
  556.1 3.9 constant_dynamic-update-slice_fusion.8
  560.0 3.8 constant_dynamic-update-slice_fusion.7
  563.8 3.8 constant_dynamic-update-slice_fusion.6
  567.6 0.0 copy-done.10
  567.6 1.9 constant_dynamic-update-slice_fusion.5
  569.5 0.0 copy-done.8
  569.5 1.9 constant_dynamic-update-slice_fusion.4
  571.4 0.0 copy-done.6
  571.4 1.9 constant_dynamic-update-slice_fusion.3
  573.3 0.0 copy-done.4
  573.4 1.9 constant_dynamic-update-slice_fusion.2
  575.2 0.0 copy-done.2
  575.2 1.9 constant_dynamic-update-slice_fusion.1
  577.1 0.0 copy-done
  577.2 1.9 constant_dynamic-update-slice_fusion
  579.0 22.4 %fusion.9 = (f32[512]{0:T(512)S(1)}, f32[6400,512]{1,0:T(8,128)}) fusion(bf16[512,2048]{1,0:T(8,128)(2,1)} %all-gather.4.cloned.1.call-done, bf16[4096,6400]{1,0:T(8,128)(2,1)} %constant_dynamic-update-slice_fusion, s32[]{:T(128)S(6)} %select_n.50), kind=kOutput, calls=%fused_computation.37 | convolution fusion | flops 13425049600 | bytes 41420804 | tf_op jit(solution)/shard_map/dot_general | solution.py:18
  601.4 5.9 pmax.7
  607.3 6.5 exponential_reduce_fusion
  613.8 18.6 %gather_fusion = f32[512]{0:T(512)S(1)} fusion(f32[512,6400]{0,1:T(8,128)} %bitcast.20, s32[512]{0:T(512)S(1)} %bitcast.19), kind=kCustom, calls=%fused_computation | custom fusion | bytes 8192 | tf_op jit(solution)/shard_map/jit(take_along_axis)/gather | solution.py:23
  632.4 0.0 copy-done.11
  632.4 5.8 all-reduce.2
  638.2 0.1 fusion.2
  638.4 0.2 dynamic-update-slice
  638.6 5.7 all-reduce
  644.3 0.2 dynamic-update-slice.1
  644.6 17.1 %all-reduce.1 = f32[800]{0:T(1024)S(1)} all-reduce(f32[800]{0:T(1024)S(1)} %dynamic-update-slice.1), channel_id=3, replica_groups=mesh['subset'=8,'vocab'=4] {'subset'}, use_global_device_ids=true, to_apply=%add.1 | all-reduce | flops 800 | bytes 6400
  661.7 4.5 sort.15
  666.2 0.0 copy-done.14
  666.2 0.7 select_reduce_fusion
  666.9 0.0 copy-done.12
  (24 shorter events, 0.1 us)
Async XLA Ops:
  7.2 570.0 %copy-start = (bf16[256,6400]{1,0:T(8,128)(2,1)S(1)}, bf16[256,6400]{1,0:T(8,128)(2,1)}, u32[]{:S(2)}) copy-start(bf16[256,6400]{1,0:T(8,128)(2,1)} %param.6) | copy-start | bytes 9830404
  7.2 571.9 %all-gather.4.cloned.1.call-start = ((), (), s32[]{:S(2)}) async-start(), calls=%async_computation | async-start | bytes 2621440 | tf_op jit(solution)/shard_map/all_gather | solution.py:8
  7.2 77.2 %collective-permute-start = (bf16[256,6400]{1,0:T(8,128)(2,1)}, bf16[256,6400]{1,0:T(8,128)(2,1)S(1)}, u32[]{:S(2)}, u32[]{:S(2)}) collective-permute-start(bf16[256,6400]{1,0:T(8,128)(2,1)} %param.6), channel_id=1, source_target_pairs={{0,4},{4,8},{8,12},{12,16},{16,20},{20,24},{24,28},{28,0},{1,5},{5... | collective-permute-start | bytes 9830408 | tf_op jit(solution)/shard_map/ppermute | solution.py:12
  84.4 1.7 copy-start.1
  86.1 74.8 %collective-permute-start.1 = (bf16[256,6400]{1,0:T(8,128)(2,1)S(1)}, bf16[256,6400]{1,0:T(8,128)(2,1)S(1)}, u32[]{:S(2)}, u32[]{:S(2)}) collective-permute-start(bf16[256,6400]{1,0:T(8,128)(2,1)S(1)} %collective-permute-done), channel_id=1, source_target_pairs={{0,4},{4,8},{8,12},{12,16},{16,20},{20,24},{24,28},{28,0},{1,5},{5... | collective-permute-start | bytes 9830408 | tf_op jit(solution)/shard_map/ppermute | solution.py:12
  160.9 1.7 copy-start.3
  162.6 73.9 %collective-permute-start.2 = (bf16[256,6400]{1,0:T(8,128)(2,1)S(1)}, bf16[256,6400]{1,0:T(8,128)(2,1)S(1)}, u32[]{:S(2)}, u32[]{:S(2)}) collective-permute-start(bf16[256,6400]{1,0:T(8,128)(2,1)S(1)} %collective-permute-done.1), channel_id=1, source_target_pairs={{0,4},{4,8},{8,12},{12,16},{16,20},{20,24},{24,28},{28,0},{1,5},{5... | collective-permute-start | bytes 9830408 | tf_op jit(solution)/shard_map/ppermute | solution.py:12
  236.5 1.7 copy-start.5
  238.2 73.1 %collective-permute-start.3 = (bf16[256,6400]{1,0:T(8,128)(2,1)S(1)}, bf16[256,6400]{1,0:T(8,128)(2,1)S(1)}, u32[]{:S(2)}, u32[]{:S(2)}) collective-permute-start(bf16[256,6400]{1,0:T(8,128)(2,1)S(1)} %collective-permute-done.2), channel_id=1, source_target_pairs={{0,4},{4,8},{8,12},{12,16},{16,20},{20,24},{24,28},{28,0},{1,5},{5... | collective-permute-start | bytes 9830408 | tf_op jit(solution)/shard_map/ppermute | solution.py:12
  311.3 1.7 copy-start.7
  313.0 72.2 %collective-permute-start.4 = (bf16[256,6400]{1,0:T(8,128)(2,1)S(1)}, bf16[256,6400]{1,0:T(8,128)(2,1)S(1)}, u32[]{:S(2)}, u32[]{:S(2)}) collective-permute-start(bf16[256,6400]{1,0:T(8,128)(2,1)S(1)} %collective-permute-done.3), channel_id=1, source_target_pairs={{0,4},{4,8},{8,12},{12,16},{16,20},{20,24},{24,28},{28,0},{1,5},{5... | collective-permute-start | bytes 9830408 | tf_op jit(solution)/shard_map/ppermute | solution.py:12
  385.2 1.7 copy-start.9
  386.9 71.5 %collective-permute-start.5 = (bf16[256,6400]{1,0:T(8,128)(2,1)S(1)}, bf16[256,6400]{1,0:T(8,128)(2,1)}, u32[]{:S(2)}, u32[]{:S(2)}) collective-permute-start(bf16[256,6400]{1,0:T(8,128)(2,1)S(1)} %collective-permute-done.4), channel_id=1, source_target_pairs={{0,4},{4,8},{8,12},{12,16},{16,20},{20,24},{24,28},{28,0},{1,5},{5... | collective-permute-start | bytes 9830408 | tf_op jit(solution)/shard_map/ppermute | solution.py:12
  458.4 70.8 %collective-permute-start.6 = (bf16[256,6400]{1,0:T(8,128)(2,1)}, bf16[256,6400]{1,0:T(8,128)(2,1)}, u32[]{:S(2)}, u32[]{:S(2)}) collective-permute-start(bf16[256,6400]{1,0:T(8,128)(2,1)} %collective-permute-done.5), channel_id=1, source_target_pairs={{0,4},{4,8},{8,12},{12,16},{16,20},{20,24},{24,28},{28,0},{1,5},{5... | collective-permute-start | bytes 9830408 | tf_op jit(solution)/shard_map/ppermute | solution.py:12
  461.7 105.9 %copy-start.10 = (bf16[256,6400]{1,0:T(8,128)(2,1)S(1)}, bf16[256,6400]{1,0:T(8,128)(2,1)}, u32[]{:S(2)}) copy-start(bf16[256,6400]{1,0:T(8,128)(2,1)} %copy-done.9) | copy-start | bytes 9830404
  461.8 107.7 %copy-start.8 = (bf16[256,6400]{1,0:T(8,128)(2,1)S(1)}, bf16[256,6400]{1,0:T(8,128)(2,1)}, u32[]{:S(2)}) copy-start(bf16[256,6400]{1,0:T(8,128)(2,1)} %copy-done.7) | copy-start | bytes 9830404
  461.8 109.7 %copy-start.6 = (bf16[256,6400]{1,0:T(8,128)(2,1)S(1)}, bf16[256,6400]{1,0:T(8,128)(2,1)}, u32[]{:S(2)}) copy-start(bf16[256,6400]{1,0:T(8,128)(2,1)} %copy-done.5) | copy-start | bytes 9830404
  461.8 111.6 %copy-start.4 = (bf16[256,6400]{1,0:T(8,128)(2,1)S(1)}, bf16[256,6400]{1,0:T(8,128)(2,1)}, u32[]{:S(2)}) copy-start(bf16[256,6400]{1,0:T(8,128)(2,1)} %copy-done.3) | copy-start | bytes 9830404
  461.8 113.5 %copy-start.2 = (bf16[256,6400]{1,0:T(8,128)(2,1)S(1)}, bf16[256,6400]{1,0:T(8,128)(2,1)}, u32[]{:S(2)}) copy-start(bf16[256,6400]{1,0:T(8,128)(2,1)} %copy-done.1) | copy-start | bytes 9830404
  579.0 53.4 %copy-start.11 = (s32[512]{0:T(512)S(1)}, s32[512]{0:T(512)}, u32[]{:S(2)}) copy-start(s32[512]{0:T(512)} %param.7) | copy-start | bytes 6148
  579.0 87.2 %copy-start.14 = (s32[8]{0:T(128)S(1)}, s32[8]{0:T(128)}, u32[]{:S(2)}) copy-start(s32[8]{0:T(128)} %param.9) | copy-start | bytes 100
  638.2 28.7 %copy-start.12 = (f32[512]{0:T(512)}, f32[512]{0:T(512)S(1)}, u32[]{:S(2)}) copy-start(f32[512]{0:T(512)S(1)} %add_subtract_fusion) | copy-start | bytes 6148
  638.3 28.6 %copy-start.13 = (f32[25]{0:T(128)}, f32[25]{0:T(128)S(1)}, u32[]{:S(2)}) copy-start(f32[25]{0:T(128)S(1)} %fusion.2) | copy-start | bytes 304
Sparse Core Ops, SparseCore 0:
  458.5 23.0 all-gather.3
